TPU v7x, 32 devices: a whole 2x2x4 slice. The times are simulated.
32 devices in a mesh: row: 4 (over y, x), col: 2 (over core), depth: 4 (over z).
Axes of the slice: x: 2, y: 2, z: 4, core: 2. Of those that a mesh axis runs over, the one named last changes fastest.
Arguments:
- a_cols: float32 [4096, 1024], P(('row', 'col')), may hold values from -16 to 24, as said below
- past_panels: float32 [4096, 2048], P(('row', 'col'), 'depth'), may hold values from -1 to 1
Outputs:
- factor: float32 [4096, 1024], P(('row', 'col'))
Inputs may be any that keep to these rules, and one draw needn't show every extreme that they name: a_cols minus past_panels times the transpose of the top 1024 rows of past_panels is the first 1024 columns of a symmetric positive definite matrix whose top block has eigenvalues between 2 and 12.
All inputs are finite; a program needn't handle non-finite values.
Results may differ from a plain program's by a relative error of at most 0.0001.
Values sent between devices are 32-bit elements.
A program may use at most 64 MiB of HBM per device.

v0:
```python
import jax
import jax.numpy as jnp
from jax import lax
from jax.sharding import PartitionSpec as P

NB = 512
STEPS = 2


def spread(array, axis, root):
    mine = lax.axis_index(axis) == root
    return lax.psum(jnp.where(mine, array, jnp.zeros_like(array)), axis)


def outer_rows(left, right):
    return lax.dot_general(
        left,
        right,
        (((1,), (1,)), ((), ())),
        precision=lax.Precision.HIGHEST,
        preferred_element_type=jnp.float32,
    )


def body(a_cols, past_panels):
    local_rows = a_cols.shape[0]
    position = lax.axis_index(("row", "col"))
    row_ids = position * local_rows + lax.broadcasted_iota(jnp.int32, (local_rows, NB), 0)
    col_ids = lax.broadcasted_iota(jnp.int32, (local_rows, NB), 1)
    result = jnp.zeros(a_cols.shape, jnp.float32)
    for section in range(STEPS):
        start = section * NB
        root = start // local_rows
        above = spread(past_panels, ("row", "col"), root)
        partial_value = outer_rows(past_panels, above)
        if section > 0:
            layer = lax.axis_index("depth")
            owned_ids = [layer + 0]
            owned_cols = [
                lax.dynamic_slice_in_dim(result, jnp.minimum(index, section - 1) * NB, NB, 1)
                for index in owned_ids
            ]
            sent_rows = jnp.stack([block for block in owned_cols])
            got_rows = spread(sent_rows, ("row", "col"), root)
            weight = (owned_ids[0] < section).astype(jnp.float32)
            partial_value = partial_value + weight * outer_rows(owned_cols[0], got_rows[0])
        summed = lax.psum(partial_value, "depth")
        update = a_cols[:, start : start + NB] - summed
        block = spread(update, ("row", "col"), root)
        diag_factor = jnp.linalg.cholesky(block)
        solved = jax.scipy.linalg.solve_triangular(diag_factor, update.T, lower=True).T
        new_panel = jnp.where(row_ids >= start + col_ids, solved, jnp.float32(0.0))
        result = result.at[:, start : start + NB].set(new_panel)
    return result


def solution(mesh):
    in_specs = (P(("row", "col"), None), P(("row", "col"), "depth"))
    out_specs = P(("row", "col"), None)
    return jax.shard_map(body, mesh=mesh, in_specs=in_specs, out_specs=out_specs, check_vma=False)
```

profile of v0, /device:TPU:0, one launch (start us, length us, event | category | flops | bytes accessed | tf_op | source)
XLA Modules:
  0.0 672.5 jit_solution(3477876616623234303)
XLA Ops:
  9.8 60.1 %all-reduce.10.cloned.1.call-done = f32[512,512]{0,1:T(8,128)} async-done(((f32[512,512]{0,1:T(8,128)}), f32[512,512]{0,1:T(8,128)}) %all-reduce.10.cloned.1.call-update) | async-done | bytes 1048592 | tf_op jit(solution)/shard_map/psum | solution.py:12
  69.9 5.7 convolution_bitcast_fusion.1
  75.7 2.7 fusion.69
  78.8 48.2 %all-reduce.12.cloned.1.call-done = f32[512,512]{0,1:T(8,128)} async-done(((f32[512,512]{0,1:T(8,128)}), f32[512,512]{0,1:T(8,128)}) %all-reduce.12.cloned.1.call-update) | async-done | bytes 1048592 | tf_op jit(solution)/shard_map/psum | solution.py:47
  127.0 2.8 broadcast_select_fusion.2
  130.8 55.3 %all-reduce.14.cloned.1.call-done = f32[512,512]{0,1:T(8,128)} async-done(((f32[512,512]{0,1:T(8,128)}), f32[512,512]{0,1:T(8,128)}) %all-reduce.14.cloned.1.call-update) | async-done | bytes 1048592 | tf_op jit(solution)/shard_map/psum | solution.py:12
  189.0 11.7 %cholesky.286 = f32[128,128]{1,0:T(8,128)S(1)} custom-call(f32[128,128]{1,0:T(8,128)S(1)} %cholesky.426), custom_call_target="Cholesky" | custom-call | tf_op jit(solution)/shard_map/jit(cholesky)/cholesky | solution.py:50
  200.8 9.8 %custom-call.27 = f32[1,128,128]{1,2,0:T(8,128)S(1)} custom-call(f32[1,128,128]{2,1,0:T(8,128)S(1)} %get-tuple-element.96), custom_call_target="InvertDiagBlocksLowerTriangular" | custom-call | tf_op jit(solution)/shard_map/jit(cholesky)/cholesky | solution.py:50
  213.2 11.7 %cholesky.305 = f32[128,128]{1,0:T(8,128)S(1)} custom-call(f32[128,128]{1,0:T(8,128)S(1)} %cholesky.430), custom_call_target="Cholesky" | custom-call | tf_op jit(solution)/shard_map/jit(cholesky)/cholesky | solution.py:50
  225.0 10.3 %custom-call.28 = f32[1,128,128]{1,2,0:T(8,128)S(1)} custom-call(f32[1,128,128]{2,1,0:T(8,128)S(1)} %get-tuple-element.93), custom_call_target="InvertDiagBlocksLowerTriangular" | custom-call | tf_op jit(solution)/shard_map/jit(cholesky)/cholesky | solution.py:50
  236.9 11.7 %cholesky.326 = f32[128,128]{1,0:T(8,128)S(1)} custom-call(f32[128,128]{1,0:T(8,128)S(1)} %cholesky.435), custom_call_target="Cholesky" | custom-call | tf_op jit(solution)/shard_map/jit(cholesky)/cholesky | solution.py:50
  249.2 9.8 %custom-call.29 = f32[1,128,128]{1,2,0:T(8,128)S(1)} custom-call(f32[1,128,128]{2,1,0:T(8,128)S(1)} %get-tuple-element.90), custom_call_target="InvertDiagBlocksLowerTriangular" | custom-call | tf_op jit(solution)/shard_map/jit(cholesky)/cholesky | solution.py:50
  260.5 11.7 %cholesky.343 = f32[128,128]{1,0:T(8,128)S(1)} custom-call(f32[128,128]{1,0:T(8,128)S(1)} %convolution_subtract_fusion.11), custom_call_target="Cholesky" | custom-call | tf_op jit(solution)/shard_map/jit(cholesky)/cholesky | solution.py:50
  277.3 11.1 %while.6 = (s32[]{:T(128)}, f32[512,512]{1,0:T(8,128)}, s32[4,2]{0,1:T(2,128)S(1)}, f32[4,128,128]{2,1,0:T(8,128)S(1)}, s32[]{:T(128)}) while((s32[]{:T(128)}, f32[512,512]{1,0:T(8,128)}, s32[4,2]{0,1:T(2,128)S(1)}, f32[4,128,128]{2,1,0:T(8,128)S(1)}, s32[]{:T(128)}) %tuple.63), condition=%wide.while_cond.2, body=%wide.while_body.2.sunk | while | flops 2 | bytes 131181 | solution.py:51
  288.4 39.3 %custom-call.30 = f32[4,128,128]{1,2,0:T(8,128)S(1)} custom-call(f32[4,128,128]{2,1,0:T(8,128)S(1)} %get-tuple-element.45), custom_call_target="InvertDiagBlocksLowerTriangular" | custom-call | tf_op jit(solution)/shard_map/jit(_solve_triangular)/triangular_solve | solution.py:51
  335.6 61.2 %all-reduce.20.cloned.1.call-done = (f32[512,512]{0,1:T(8,128)}, f32[512,512]{0,1:T(8,128)}) async-done(((f32[512,512]{0,1:T(8,128)}, f32[512,512]{0,1:T(8,128)}), (f32[512,512]{0,1:T(8,128)}, f32[512,512]{0,1:T(8,128)})) %all-reduce.20.cloned.1.call-update) | async-done | bytes 2097168 | tf_op jit(solution)/shard_map/psum | solution.py:12
  396.8 4.8 convolution_bitcast_fusion
  401.6 2.9 fusion
  405.1 50.5 %all-reduce.16.cloned.1.call-done = f32[512,512]{0,1:T(8,128)} async-done(((f32[512,512]{0,1:T(8,128)}), f32[512,512]{0,1:T(8,128)}) %all-reduce.16.cloned.1.call-update) | async-done | bytes 1048592 | tf_op jit(solution)/shard_map/psum | solution.py:47
  455.6 2.8 broadcast_select_fusion
  458.4 56.2 %all-reduce.18.cloned.1.call-done = f32[512,512]{0,1:T(8,128)} async-done(((f32[512,512]{0,1:T(8,128)}), f32[512,512]{0,1:T(8,128)}) %all-reduce.18.cloned.1.call-update) | async-done | bytes 1048592 | tf_op jit(solution)/shard_map/psum | solution.py:12
  517.5 11.7 %cholesky.358 = f32[128,128]{1,0:T(8,128)S(1)} custom-call(f32[128,128]{1,0:T(8,128)S(1)} %cholesky.439), custom_call_target="Cholesky" | custom-call | tf_op jit(solution)/shard_map/jit(cholesky)/cholesky | solution.py:50
  529.4 9.8 %custom-call.31 = f32[1,128,128]{1,2,0:T(8,128)S(1)} custom-call(f32[1,128,128]{2,1,0:T(8,128)S(1)} %get-tuple-element.86), custom_call_target="InvertDiagBlocksLowerTriangular" | custom-call | tf_op jit(solution)/shard_map/jit(cholesky)/cholesky | solution.py:50
  541.7 11.7 %cholesky.377 = f32[128,128]{1,0:T(8,128)S(1)} custom-call(f32[128,128]{1,0:T(8,128)S(1)} %cholesky.443), custom_call_target="Cholesky" | custom-call | tf_op jit(solution)/shard_map/jit(cholesky)/cholesky | solution.py:50
  554.8 10.2 %custom-call.32 = f32[1,128,128]{1,2,0:T(8,128)S(1)} custom-call(f32[1,128,128]{2,1,0:T(8,128)S(1)} %get-tuple-element.83), custom_call_target="InvertDiagBlocksLowerTriangular" | custom-call | tf_op jit(solution)/shard_map/jit(cholesky)/cholesky | solution.py:50
  566.6 11.7 %cholesky.398 = f32[128,128]{1,0:T(8,128)S(1)} custom-call(f32[128,128]{1,0:T(8,128)S(1)} %cholesky.448), custom_call_target="Cholesky" | custom-call | tf_op jit(solution)/shard_map/jit(cholesky)/cholesky | solution.py:50
  579.0 9.8 %custom-call.33 = f32[1,128,128]{1,2,0:T(8,128)S(1)} custom-call(f32[1,128,128]{2,1,0:T(8,128)S(1)} %get-tuple-element.80), custom_call_target="InvertDiagBlocksLowerTriangular" | custom-call | tf_op jit(solution)/shard_map/jit(cholesky)/cholesky | solution.py:50
  590.3 11.8 %cholesky.415 = f32[128,128]{1,0:T(8,128)S(1)} custom-call(f32[128,128]{1,0:T(8,128)S(1)} %convolution_subtract_fusion.10), custom_call_target="Cholesky" | custom-call | tf_op jit(solution)/shard_map/jit(cholesky)/cholesky | solution.py:50
  606.4 11.7 %while.7 = (s32[]{:T(128)}, f32[512,512]{1,0:T(8,128)}, s32[4,2]{0,1:T(2,128)S(1)}, f32[4,128,128]{2,1,0:T(8,128)S(1)}, s32[]{:T(128)}) while((s32[]{:T(128)}, f32[512,512]{1,0:T(8,128)}, s32[4,2]{0,1:T(2,128)S(1)}, f32[4,128,128]{2,1,0:T(8,128)S(1)}, s32[]{:T(128)}) %tuple.82), condition=%wide.while_cond.2.clone, body=%wide.while_body.2.clone.sunk | while | flops 2 | bytes 131181 | solution.py:51
  607.1 2.3 bitcast_dynamic-update-slice_fusion.5
  610.0 2.3 bitcast_dynamic-update-slice_fusion.5
  618.1 39.3 %custom-call.34 = f32[4,128,128]{1,2,0:T(8,128)S(1)} custom-call(f32[4,128,128]{2,1,0:T(8,128)S(1)} %get-tuple-element.46), custom_call_target="InvertDiagBlocksLowerTriangular" | custom-call | tf_op jit(solution)/shard_map/jit(_solve_triangular)/triangular_solve | solution.py:51
  (123 shorter events, 63.3 us)
Async XLA Ops:
  6.5 63.4 %all-reduce.10.cloned.1.call-start = ((), (), s32[]{:S(2)}) async-start(), calls=%async_computation | async-start | bytes 2097152 | tf_op jit(solution)/shard_map/psum | solution.py:12
  8.1 61.8 %copy-start = (f32[512,512]{1,0:T(8,128)S(1)}, f32[512,512]{1,0:T(8,128)}, u32[]{:S(2)}) copy-start(f32[512,512]{1,0:T(8,128)} %param.10) | copy-start | bytes 3145732
  9.8 117.2 %all-reduce.12.cloned.1.call-start = ((), (), s32[]{:S(2)}) async-start(), calls=%async_computation.1 | async-start | bytes 2097152 | tf_op jit(solution)/shard_map/psum | solution.py:47
  75.7 110.4 %all-reduce.14.cloned.1.call-start = ((), (), s32[]{:S(2)}) async-start(), calls=%async_computation.2 | async-start | bytes 2097152 | tf_op jit(solution)/shard_map/psum | solution.py:12
  129.8 267.0 %all-reduce.20.cloned.1.call-start = ((), (), s32[]{:S(2)}) async-start(), calls=%async_computation.5 | async-start | bytes 4194304 | tf_op jit(solution)/shard_map/psum | solution.py:12
  186.1 1.7 copy-start.1
  188.0 1.0 copy-start.7
  236.9 90.9 %copy-start.3 = (f32[512,512]{1,0:T(8,128)S(1)}, f32[512,512]{1,0:T(8,128)}, u32[]{:S(2)}) copy-start(f32[512,512]{1,0:T(8,128)} %get-tuple-element.72) | copy-start | bytes 3145732
  335.5 120.1 %all-reduce.16.cloned.1.call-start = ((), (), s32[]{:S(2)}) async-start(), calls=%async_computation.3 | async-start | bytes 2097152 | tf_op jit(solution)/shard_map/psum | solution.py:47
  396.8 4.8 copy-start.8
  401.6 3.2 copy-start.5
  404.5 110.1 %all-reduce.18.cloned.1.call-start = ((), (), s32[]{:S(2)}) async-start(), calls=%async_computation.4 | async-start | bytes 2097152 | tf_op jit(solution)/shard_map/psum | solution.py:12
  514.6 1.7 copy-start.2
  516.5 1.0 copy-start.6
  566.6 90.9 %copy-start.4 = (f32[512,512]{1,0:T(8,128)S(1)}, f32[512,512]{1,0:T(8,128)}, u32[]{:S(2)}) copy-start(f32[512,512]{1,0:T(8,128)} %get-tuple-element.70) | copy-start | bytes 3145732
Sparse Core Ops, SparseCore 0:
  10.5 59.4 all-reduce.9
  75.8 51.1 all-reduce.11
  130.1 55.9 all-reduce.13
  335.6 61.0 all-reduce.19
  404.6 50.9 all-reduce.15
  458.6 55.9 all-reduce.17
where the time goes:
time: 678 us; the launch traced here: 672 us
  waiting for transfers between devices  332 us (49%)
  other arithmetic  250 us (37%)
  matrix products  35.9 us (5%)
  local copies, waits for them, and re-layouts  34.9 us (5%)
  between operations  19.2 us (3%)
    psum x4, waiting for transfers between devices, spread(): return lax.psum(jnp.where(mine, array, jnp.zeros_like(array)), axis)  233 us
    another operation x29, other arithmetic, body(): diag_factor = jnp.linalg.cholesky(block)  158 us
    psum x2, waiting for transfers between devices, body(): summed = lax.psum(partial_value, 'depth')  98.7 us
    another operation x5, other arithmetic, body(): jax.scipy.linalg.solve_triangular(diag_factor, update.T, lower=True)  81 us
    another operation x27, local copies, waits for them, and re-layouts, body(): jax.scipy.linalg.solve_triangular(diag_factor, update.T, lower=True)  22.6 us
  transfers between devices with their start and end apart: 6, of which 6 were waited for; matrix products, arithmetic and copies ran while one was open for 1% of the time, Pallas kernels for 0%

commit v1 on v0

--- a/solution.py
+++ b/solution.py
@@ -44,7 +44,9 @@
             got_rows = spread(sent_rows, ("row", "col"), root)
             weight = (owned_ids[0] < section).astype(jnp.float32)
             partial_value = partial_value + weight * outer_rows(owned_cols[0], got_rows[0])
-        summed = lax.psum(partial_value, "depth")
+        summed = partial_value
+        for hop in (1, 2):
+            summed = summed + lax.ppermute(summed, "depth", [(dev, dev ^ hop) for dev in range(4)])
         update = a_cols[:, start : start + NB] - summed
         block = spread(update, ("row", "col"), root)
         diag_factor = jnp.linalg.cholesky(block)

time: 678 us -> 717 us (1.058)
  waiting for transfers between devices: 332 us -> 363 us
  starting transfers between devices: 0.42 us -> 8.02 us
    ppermute x0 -> x4, waiting for transfers between devices: none -> 129 us  [body(): lax.ppermute(summed, 'depth', [(dev, dev ^ hop) for dev in range(4)])]
    psum x2 -> x0, waiting for transfers between devices: 98.7 us -> none  [body(): summed = lax.psum(partial_value, 'depth')]
    ppermute x0 -> x4, starting transfers between devices: none -> 7.89 us  [body(): lax.ppermute(summed, 'depth', [(dev, dev ^ hop) for dev in range(4)])]
  transfers between devices with their start and end apart: 6 -> 8, of which waited for: 6 -> 8; matrix products, arithmetic and copies ran while one was open for 1% -> 1% of each run, Pallas kernels for 0% -> 0%
where the time goes in v1:
time: 717 us; the launch traced here: 711 us
  waiting for transfers between devices  363 us (51%)
  other arithmetic  251 us (35%)
  local copies, waits for them, and re-layouts  35.9 us (5%)
  matrix products  33.9 us (5%)
  between operations  19 us (3%)
  starting transfers between devices  8.02 us (1%)
    psum x4, waiting for transfers between devices, spread(): return lax.psum(jnp.where(mine, array, jnp.zeros_like(array)), axis)  234 us
    another operation x29, other arithmetic, body(): diag_factor = jnp.linalg.cholesky(block)  158 us
    ppermute x4, waiting for transfers between devices, body(): lax.ppermute(summed, 'depth', [(dev, dev ^ hop) for dev in range(4)])  129 us
    another operation x5, other arithmetic, body(): jax.scipy.linalg.solve_triangular(diag_factor, update.T, lower=True)  81.2 us
    another operation x27, local copies, waits for them, and re-layouts, body(): jax.scipy.linalg.solve_triangular(diag_factor, update.T, lower=True)  22.6 us
  transfers between devices with their start and end apart: 8, of which 8 were waited for; matrix products, arithmetic and copies ran while one was open for 1% of the time, Pallas kernels for 0%

profile of v1, /device:TPU:0, one launch (start us, length us, event | category | flops | bytes accessed | tf_op | source)
XLA Modules:
  0.0 711.5 jit_solution(1821003272218856243)
XLA Ops:
  9.9 60.1 %all-reduce.8.cloned.1.call-done = f32[512,512]{0,1:T(8,128)} async-done(((f32[512,512]{0,1:T(8,128)}), f32[512,512]{0,1:T(8,128)}) %all-reduce.8.cloned.1.call-update) | async-done | bytes 1048592 | tf_op jit(solution)/shard_map/psum | solution.py:12
  69.9 4.7 convolution_bitcast_fusion.1
  76.1 22.6 %collective-permute-done = f32[512,512]{0,1:T(8,128)S(1)} collective-permute-done((f32[512,512]{0,1:T(8,128)S(1)}, f32[512,512]{0,1:T(8,128)S(1)}, u32[]{:S(2)}, u32[]{:S(2)}) %collective-permute-start) | collective-permute-done | bytes 1048608 | tf_op jit(solution)/shard_map/ppermute | solution.py:49
  99.0 2.5 collective-permute-start.1
  104.5 41.1 %collective-permute-done.1 = f32[512,512]{0,1:T(8,128)} collective-permute-done((f32[512,512]{0,1:T(8,128)S(1)}, f32[512,512]{0,1:T(8,128)}, u32[]{:S(2)}, u32[]{:S(2)}) %collective-permute-start.1) | collective-permute-done | bytes 1048608 | tf_op jit(solution)/shard_map/ppermute | solution.py:49
  145.7 2.9 broadcast_select_fusion.2
  149.8 55.3 %all-reduce.10.cloned.1.call-done = f32[512,512]{0,1:T(8,128)} async-done(((f32[512,512]{0,1:T(8,128)}), f32[512,512]{0,1:T(8,128)}) %all-reduce.10.cloned.1.call-update) | async-done | bytes 1048592 | tf_op jit(solution)/shard_map/psum | solution.py:12
  208.0 11.7 %cholesky.286 = f32[128,128]{1,0:T(8,128)S(1)} custom-call(f32[128,128]{1,0:T(8,128)S(1)} %cholesky.426), custom_call_target="Cholesky" | custom-call | tf_op jit(solution)/shard_map/jit(cholesky)/cholesky | solution.py:52
  219.9 9.8 %custom-call.27 = f32[1,128,128]{1,2,0:T(8,128)S(1)} custom-call(f32[1,128,128]{2,1,0:T(8,128)S(1)} %get-tuple-element.96), custom_call_target="InvertDiagBlocksLowerTriangular" | custom-call | tf_op jit(solution)/shard_map/jit(cholesky)/cholesky | solution.py:52
  232.2 11.7 %cholesky.305 = f32[128,128]{1,0:T(8,128)S(1)} custom-call(f32[128,128]{1,0:T(8,128)S(1)} %cholesky.430), custom_call_target="Cholesky" | custom-call | tf_op jit(solution)/shard_map/jit(cholesky)/cholesky | solution.py:52
  244.0 10.0 %custom-call.28 = f32[1,128,128]{1,2,0:T(8,128)S(1)} custom-call(f32[1,128,128]{2,1,0:T(8,128)S(1)} %get-tuple-element.93), custom_call_target="InvertDiagBlocksLowerTriangular" | custom-call | tf_op jit(solution)/shard_map/jit(cholesky)/cholesky | solution.py:52
  255.5 11.7 %cholesky.326 = f32[128,128]{1,0:T(8,128)S(1)} custom-call(f32[128,128]{1,0:T(8,128)S(1)} %cholesky.435), custom_call_target="Cholesky" | custom-call | tf_op jit(solution)/shard_map/jit(cholesky)/cholesky | solution.py:52
  267.9 9.8 %custom-call.29 = f32[1,128,128]{1,2,0:T(8,128)S(1)} custom-call(f32[1,128,128]{2,1,0:T(8,128)S(1)} %get-tuple-element.90), custom_call_target="InvertDiagBlocksLowerTriangular" | custom-call | tf_op jit(solution)/shard_map/jit(cholesky)/cholesky | solution.py:52
  279.1 11.7 %cholesky.343 = f32[128,128]{1,0:T(8,128)S(1)} custom-call(f32[128,128]{1,0:T(8,128)S(1)} %convolution_subtract_fusion.5), custom_call_target="Cholesky" | custom-call | tf_op jit(solution)/shard_map/jit(cholesky)/cholesky | solution.py:52
  296.3 11.1 %while.6 = (s32[]{:T(128)}, f32[512,512]{1,0:T(8,128)}, s32[4,2]{0,1:T(2,128)S(1)}, f32[4,128,128]{2,1,0:T(8,128)S(1)}, s32[]{:T(128)}) while((s32[]{:T(128)}, f32[512,512]{1,0:T(8,128)}, s32[4,2]{0,1:T(2,128)S(1)}, f32[4,128,128]{2,1,0:T(8,128)S(1)}, s32[]{:T(128)}) %tuple.63), condition=%wide.while_cond.2, body=%wide.while_body.2.sunk | while | flops 2 | bytes 131181 | solution.py:53
  307.4 39.3 %custom-call.30 = f32[4,128,128]{1,2,0:T(8,128)S(1)} custom-call(f32[4,128,128]{2,1,0:T(8,128)S(1)} %get-tuple-element.45), custom_call_target="InvertDiagBlocksLowerTriangular" | custom-call | tf_op jit(solution)/shard_map/jit(_solve_triangular)/triangular_solve | solution.py:53
  354.5 61.2 %all-reduce.14.cloned.1.call-done = (f32[512,512]{0,1:T(8,128)}, f32[512,512]{0,1:T(8,128)}) async-done(((f32[512,512]{0,1:T(8,128)}, f32[512,512]{0,1:T(8,128)}), (f32[512,512]{0,1:T(8,128)}, f32[512,512]{0,1:T(8,128)})) %all-reduce.14.cloned.1.call-update) | async-done | bytes 2097168 | tf_op jit(solution)/shard_map/psum | solution.py:12
  415.7 4.8 convolution_bitcast_fusion
  423.9 22.3 %collective-permute-done.2 = f32[512,512]{0,1:T(8,128)S(1)} collective-permute-done((f32[512,512]{0,1:T(8,128)S(1)}, f32[512,512]{0,1:T(8,128)S(1)}, u32[]{:S(2)}, u32[]{:S(2)}) %collective-permute-start.2) | collective-permute-done | bytes 1048608 | tf_op jit(solution)/shard_map/ppermute | solution.py:49
  446.5 2.5 collective-permute-start.3
  450.3 42.6 %collective-permute-done.3 = f32[512,512]{0,1:T(8,128)} collective-permute-done((f32[512,512]{0,1:T(8,128)S(1)}, f32[512,512]{0,1:T(8,128)}, u32[]{:S(2)}, u32[]{:S(2)}) %collective-permute-start.3) | collective-permute-done | bytes 1048608 | tf_op jit(solution)/shard_map/ppermute | solution.py:49
  492.9 3.3 broadcast_select_fusion
  496.2 57.9 %all-reduce.12.cloned.1.call-done = f32[512,512]{0,1:T(8,128)} async-done(((f32[512,512]{0,1:T(8,128)}), f32[512,512]{0,1:T(8,128)}) %all-reduce.12.cloned.1.call-update) | async-done | bytes 1048592 | tf_op jit(solution)/shard_map/psum | solution.py:12
  556.9 11.7 %cholesky.358 = f32[128,128]{1,0:T(8,128)S(1)} custom-call(f32[128,128]{1,0:T(8,128)S(1)} %cholesky.439), custom_call_target="Cholesky" | custom-call | tf_op jit(solution)/shard_map/jit(cholesky)/cholesky | solution.py:52
  568.8 10.0 %custom-call.31 = f32[1,128,128]{1,2,0:T(8,128)S(1)} custom-call(f32[1,128,128]{2,1,0:T(8,128)S(1)} %get-tuple-element.86), custom_call_target="InvertDiagBlocksLowerTriangular" | custom-call | tf_op jit(solution)/shard_map/jit(cholesky)/cholesky | solution.py:52
  581.3 11.7 %cholesky.377 = f32[128,128]{1,0:T(8,128)S(1)} custom-call(f32[128,128]{1,0:T(8,128)S(1)} %cholesky.443), custom_call_target="Cholesky" | custom-call | tf_op jit(solution)/shard_map/jit(cholesky)/cholesky | solution.py:52
  594.4 9.8 %custom-call.32 = f32[1,128,128]{1,2,0:T(8,128)S(1)} custom-call(f32[1,128,128]{2,1,0:T(8,128)S(1)} %get-tuple-element.83), custom_call_target="InvertDiagBlocksLowerTriangular" | custom-call | tf_op jit(solution)/shard_map/jit(cholesky)/cholesky | solution.py:52
  605.8 11.7 %cholesky.398 = f32[128,128]{1,0:T(8,128)S(1)} custom-call(f32[128,128]{1,0:T(8,128)S(1)} %cholesky.448), custom_call_target="Cholesky" | custom-call | tf_op jit(solution)/shard_map/jit(cholesky)/cholesky | solution.py:52
  618.2 10.0 %custom-call.33 = f32[1,128,128]{1,2,0:T(8,128)S(1)} custom-call(f32[1,128,128]{2,1,0:T(8,128)S(1)} %get-tuple-element.80), custom_call_target="InvertDiagBlocksLowerTriangular" | custom-call | tf_op jit(solution)/shard_map/jit(cholesky)/cholesky | solution.py:52
  629.7 11.7 %cholesky.415 = f32[128,128]{1,0:T(8,128)S(1)} custom-call(f32[128,128]{1,0:T(8,128)S(1)} %convolution_subtract_fusion.4), custom_call_target="Cholesky" | custom-call | tf_op jit(solution)/shard_map/jit(cholesky)/cholesky | solution.py:52
  645.7 11.7 %while.7 = (s32[]{:T(128)}, f32[512,512]{1,0:T(8,128)}, s32[4,2]{0,1:T(2,128)S(1)}, f32[4,128,128]{2,1,0:T(8,128)S(1)}, s32[]{:T(128)}) while((s32[]{:T(128)}, f32[512,512]{1,0:T(8,128)}, s32[4,2]{0,1:T(2,128)S(1)}, f32[4,128,128]{2,1,0:T(8,128)S(1)}, s32[]{:T(128)}) %tuple.78), condition=%wide.while_cond.2.clone, body=%wide.while_body.2.clone.sunk | while | flops 2 | bytes 131181 | solution.py:53
  657.4 39.3 %custom-call.34 = f32[4,128,128]{1,2,0:T(8,128)S(1)} custom-call(f32[4,128,128]{2,1,0:T(8,128)S(1)} %get-tuple-element.46), custom_call_target="InvertDiagBlocksLowerTriangular" | custom-call | tf_op jit(solution)/shard_map/jit(_solve_triangular)/triangular_solve | solution.py:53
  (129 shorter events, 77.0 us)
Async XLA Ops:
  6.5 63.4 %all-reduce.8.cloned.1.call-start = ((), (), s32[]{:S(2)}) async-start(), calls=%async_computation | async-start | bytes 2097152 | tf_op jit(solution)/shard_map/psum | solution.py:12
  8.1 61.8 %copy-start = (f32[512,512]{1,0:T(8,128)S(1)}, f32[512,512]{1,0:T(8,128)}, u32[]{:S(2)}) copy-start(f32[512,512]{1,0:T(8,128)} %param.10) | copy-start | bytes 3145732
  9.8 195.3 %all-reduce.10.cloned.1.call-start = ((), (), s32[]{:S(2)}) async-start(), calls=%async_computation.1 | async-start | bytes 2097152 | tf_op jit(solution)/shard_map/psum | solution.py:12
  74.6 26.8 %copy-start.8 = (f32[512,1024]{1,0:T(8,128)S(1)}, f32[512,1024]{1,0:T(8,128)}, u32[]{:S(2)}) copy-start(f32[512,1024]{1,0:T(8,128)} %param.9) | copy-start | bytes 6291460
  74.7 24.1 %collective-permute-start = (f32[512,512]{0,1:T(8,128)S(1)}, f32[512,512]{0,1:T(8,128)S(1)}, u32[]{:S(2)}, u32[]{:S(2)}) collective-permute-start(f32[512,512]{0,1:T(8,128)S(1)} %convolution_bitcast_fusion.1), channel_id=1, source_target_pairs={{0,1},{1,0},{2,3},{3,2},{4,5},{5,4},{6,7},{7,6},{8,9},{9,8},{10,11... | collective-permute-start | bytes 3145736 | tf_op jit(solution)/shard_map/ppermute | solution.py:49
  99.0 46.7 %collective-permute-start.1 = (f32[512,512]{0,1:T(8,128)S(1)}, f32[512,512]{0,1:T(8,128)}, u32[]{:S(2)}, u32[]{:S(2)}) collective-permute-start(f32[512,512]{0,1:T(8,128)S(1)} %add.91), channel_id=1, source_target_pairs={{0,2},{1,3},{2,0},{3,1},{4,6},{5,7},{6,4},{7,5},{8,10},{9,11},{10,... | collective-permute-start | bytes 3145736 | tf_op jit(solution)/shard_map/ppermute | solution.py:49
  148.6 267.1 %all-reduce.14.cloned.1.call-start = ((), (), s32[]{:S(2)}) async-start(), calls=%async_computation.3 | async-start | bytes 4194304 | tf_op jit(solution)/shard_map/psum | solution.py:12
  205.1 1.7 copy-start.1
  207.0 1.0 copy-start.7
  255.5 91.2 %copy-start.3 = (f32[512,512]{1,0:T(8,128)S(1)}, f32[512,512]{1,0:T(8,128)}, u32[]{:S(2)}) copy-start(f32[512,512]{1,0:T(8,128)} %get-tuple-element.72) | copy-start | bytes 3145732
  354.5 199.6 %all-reduce.12.cloned.1.call-start = ((), (), s32[]{:S(2)}) async-start(), calls=%async_computation.2 | async-start | bytes 2097152 | tf_op jit(solution)/shard_map/psum | solution.py:12
  415.7 4.8 copy-start.9
  422.5 26.5 %copy-start.5 = (f32[512,512]{1,0:T(8,128)S(1)}, f32[512,512]{1,0:T(8,128)}, u32[]{:S(2)}) copy-start(f32[512,512]{1,0:T(8,128)} %get-tuple-element.74) | copy-start | bytes 3145732
  422.5 23.8 %collective-permute-start.2 = (f32[512,512]{0,1:T(8,128)S(1)}, f32[512,512]{0,1:T(8,128)S(1)}, u32[]{:S(2)}, u32[]{:S(2)}) collective-permute-start(f32[512,512]{0,1:T(8,128)S(1)} %fusion), channel_id=1, source_target_pairs={{0,1},{1,0},{2,3},{3,2},{4,5},{5,4},{6,7},{7,6},{8,9},{9,8},{10,11... | collective-permute-start | bytes 3145736 | tf_op jit(solution)/shard_map/ppermute | solution.py:49
  446.5 46.4 %collective-permute-start.3 = (f32[512,512]{0,1:T(8,128)S(1)}, f32[512,512]{0,1:T(8,128)}, u32[]{:S(2)}, u32[]{:S(2)}) collective-permute-start(f32[512,512]{0,1:T(8,128)S(1)} %add.97), channel_id=1, source_target_pairs={{0,2},{1,3},{2,0},{3,1},{4,6},{5,7},{6,4},{7,5},{8,10},{9,11},{10,... | collective-permute-start | bytes 3145736 | tf_op jit(solution)/shard_map/ppermute | solution.py:49
  554.1 1.7 copy-start.2
  556.0 1.0 copy-start.6
  605.8 91.0 %copy-start.4 = (f32[512,512]{1,0:T(8,128)S(1)}, f32[512,512]{1,0:T(8,128)}, u32[]{:S(2)}) copy-start(f32[512,512]{1,0:T(8,128)} %get-tuple-element.70) | copy-start | bytes 3145732
Sparse Core Ops, SparseCore 0:
  10.5 59.4 all-reduce.7
  148.7 56.3 all-reduce.9
  354.6 61.0 all-reduce.13
  496.3 57.7 all-reduce.11
